TPU v7x, 32 devices: a whole 2x2x4 slice. The times are simulated.
32 devices in a mesh: path: 4 (over z), tm: 8 (over y, x, core).
Axes of the slice: x: 2, y: 2, z: 4, core: 2. Of those that a mesh axis runs over, the one named last changes fastest.
Arguments:
- values: bfloat16 [2048, 16, 2048], P('path', 'tm'), may hold values from -5 to 5
- hazard: float32 [16, 2048], P('tm', 'path'), may hold values from 0.0125 to 0.1875
- spread: float32 [16], P('tm'), may hold values from 0.3 to 3
- trade_set: int32 [2048], replicated, may hold values from 0 to 255
Outputs:
- pathwise_fva: float32 [2048, 256], P(('path', 'tm'))
- set_fva: float32 [256], P(('path', 'tm'))
All inputs are finite; a program needn't handle non-finite values.
Results may differ from a plain program's by a relative error of at most 0.0003.
Values sent between devices are 32-bit elements; how exact they have to be, the bound alone decides.
A program may use at most 64 MiB of HBM per device.

v0:
```python
import functools

import jax
import jax.numpy as jnp
from jax import lax
from jax.experimental import pallas as pl
from jax.experimental.pallas import tpu as pltpu
from jax.sharding import PartitionSpec as P

SETS = 256
CHUNK_PATHS = 128
LANES = 128
MESH = pl.DeviceIdType.MESH


def kernel(
    n_path, n_tm, values, hazard_in, spread, trade_in, out, set_out,
    vbuf, ts, oh, hz, nbuf, wt, contrib, pair, comb, recv, hbuf, pcol, erow, ecol, row_a, rows_a,
    load_sem, small_sem, h_send, h_recv, p_send, p_recv, b_send, b_recv, a_send, a_recv, ready,
):
    paths, dates, trades = values.shape
    own = paths // n_tm
    chunks = paths // CHUNK_PATHS
    per = n_tm // chunks
    n_all = n_path * n_tm
    chips = n_tm // 2
    path_at, me = lax.axis_index("path"), lax.axis_index("tm")
    flat = path_at * n_tm + me
    chip, core = lax.div(me, 2), lax.rem(me, 2)
    partner = me + 1 - 2 * core
    peers = [lax.rem(me + k, n_tm) for k in range(1, n_tm)]
    path_peers = [lax.rem(path_at + k, n_path) for k in range(1, n_path)]
    rows = CHUNK_PATHS * dates
    my_chunk = lax.div(me, per)
    first = [lax.rem(my_chunk + 1 + i, chunks) for i in range(chunks)]
    flat_values = values.reshape(paths * dates, trades)

    def load(i):
        span = pl.ds(pl.multiple_of(first[i] * rows, rows), rows)
        return pltpu.make_async_copy(flat_values.at[span], vbuf.at[span], load_sem.at[i])

    copy_trades = pltpu.make_async_copy(trade_in, ts, small_sem.at[0])
    copy_hazard = pltpu.make_async_copy(hazard_in, hz, small_sem.at[1])
    copy_trades.start()
    copy_hazard.start()
    for i in range(chunks):
        load(i).start()

    barrier = pltpu.get_barrier_semaphore()

    for other in peers:
        pl.semaphore_signal(barrier, inc=1, device_id=(path_at, other), device_id_type=MESH)
    for other in path_peers:
        pl.semaphore_signal(barrier, inc=1, device_id=(other, me), device_id_type=MESH)

    copy_trades.wait()
    set_at = lax.broadcasted_iota(jnp.int32, (SETS, LANES), 0)
    for block in range(trades // LANES):
        same = jnp.broadcast_to(ts[pl.ds(block, 1), :], (SETS, LANES)) == set_at
        oh[:, pl.ds(block * LANES, LANES)] = jnp.where(same, 1.0, 0.0).astype(jnp.bfloat16)

    copy_hazard.wait()
    total = jnp.zeros((1, paths), jnp.float32)
    weight_rows = []
    scale = 1.0 / (dates * n_tm)
    for d in range(dates):
        total = total + hz[pl.ds(d, 1), :]
        weight_rows.append((spread[d] * scale) * jnp.exp(-total))
    weight_rows.append(jnp.zeros((8 - dates, paths), jnp.float32))
    wt[...] = jnp.transpose(jnp.concatenate(weight_rows, axis=0))
    hbuf[me] = hz[...]

    def remote(src, dst, send, recv_at, device):
        return pltpu.make_async_remote_copy(
            src_ref=src, dst_ref=dst, send_sem=send, recv_sem=recv_at, device_id=device, device_id_type=MESH
        )

    def own_rows(index):
        return pl.ds(pl.multiple_of(index * own, own), own)

    def hazard_copy(other, slot):
        return remote(hz, hbuf.at[slot], h_send.at[other], h_recv.at[slot], (path_at, other))

    def pair_copy(q):
        theirs = contrib.at[own_rows(q * 2 + 1 - core)]
        return remote(theirs, pair.at[q], p_send.at[q], p_recv.at[q], (path_at, partner))

    def block_copy(q, slot):
        return remote(comb.at[q], recv.at[slot], b_send.at[q], b_recv.at[slot], (path_at, q * 2 + core))

    targets = [(z, other) for z in path_peers for other in peers + [me]]
    targets += [(path_at, other) for other in peers]

    def set_row(z, other, slot):
        return remote(row_a, rows_a.at[slot], a_send.at[z * n_tm + other], a_recv.at[slot], (z, other))

    def combine(q):
        pair_copy(q).wait_recv()
        mine = own_rows(q * 2 + core)
        factor = pcol[mine, :]
        return factor[:, 0:1] * contrib[mine, :] + factor[:, 1:2] * pair[q]

    def forward(i):
        for k in range(per // 2):
            q = first[i] * (per // 2) + k
            comb[q] = combine(q)
            block_copy(q, chip).start()

    for i in range(chunks):
        load(i).wait()
        span = pl.ds(pl.multiple_of(first[i] * rows, rows), rows)
        netted = lax.dot_general(
            vbuf[span, :], oh[...], (((1,), (1,)), ((), ())), preferred_element_type=jnp.float32
        )
        for h in range(SETS // LANES):
            nbuf[i, h] = netted[:, h * LANES : (h + 1) * LANES]
        path_span = pl.ds(pl.multiple_of(first[i] * CHUNK_PATHS, CHUNK_PATHS), CHUNK_PATHS)
        weight = wt[path_span, :]
        for h in range(SETS // LANES):
            part = None
            for d in range(dates):
                picked = nbuf[i, h, pl.ds(d, CHUNK_PATHS, stride=dates), :]
                term = weight[:, d : d + 1] * jnp.maximum(picked, 0.0)
                part = term if part is None else part + term
            contrib[path_span, pl.ds(h * LANES, LANES)] = part
        if i == 0:
            pl.semaphore_wait(barrier, n_tm - 1 + n_path - 1)
            for other in path_peers:
                pl.semaphore_signal(ready, inc=1, device_id=(other, me), device_id_type=MESH)
            hazard_copy(partner, me).start()
            for other in peers:
                @pl.when(other != partner)
                def _():
                    hazard_copy(other, me).start()
        for k in range(per // 2):
            pair_copy(first[i] * (per // 2) + k).start()
        if i == 1:
            hazard_copy(partner, partner).wait_recv()
            block = jnp.sum(hbuf[me - core], axis=0, keepdims=True)
            late = core.astype(jnp.float32)
            factors = [jnp.exp(-late * block), jnp.exp((late - 1.0) * block)]
            factors.append(jnp.zeros((6, paths), jnp.float32))
            pcol[...] = jnp.transpose(jnp.concatenate(factors, axis=0))
        if 1 <= i < chunks - 1:
            forward(i - 1)

    for other in peers:
        @pl.when(other != partner)
        def _():
            hazard_copy(other, other).wait_recv()
    block_sums = jnp.sum(hbuf[...], axis=1)
    before = jnp.zeros((1, paths), jnp.float32)
    prefix = []
    for k in range(n_tm):
        prefix.append(before)
        before = before + block_sums[k : k + 1, :]
    earlier = jnp.exp(-jnp.concatenate(prefix, axis=0))
    erow[...] = earlier
    ecol[...] = jnp.transpose(earlier)
    mine = jnp.broadcast_to(erow[pl.ds(me, 1), :], (8, paths))
    set_part = jnp.dot(
        mine, contrib[...], precision=lax.Precision.HIGHEST, preferred_element_type=jnp.float32
    )
    row_a[...] = set_part[:1] * (1.0 / (paths * n_path))
    pl.semaphore_wait(ready, n_path - 1)
    for z, other in targets:
        set_row(z, other, flat).start()
    forward(chunks - 2)
    own_chips = [my_chunk * (per // 2) + lax.rem(lax.rem(chip, per // 2) + k, per // 2) for k in range(per // 2)]
    for q in own_chips[1:]:
        comb[q] = combine(q)
        block_copy(q, chip).start()

    rows_a[flat] = row_a[...]
    recv[chip] = combine(own_chips[0])

    other_chips = [lax.rem(chip + k, chips) for k in range(1, chips)]
    for q in other_chips:
        block_copy(q, q).wait_recv()
    factor = ecol[own_rows(me), :]
    result = None
    for k in range(chips):
        term = factor[:, 2 * k : 2 * k + 1] * recv[k]
        result = term if result is None else result + term
    out[...] = result

    for z, other in targets:
        set_row(z, other, z * n_tm + other).wait_recv()
    sums = jnp.broadcast_to(jnp.sum(rows_a[...], axis=0), (8, SETS))
    share = SETS // n_all
    turned = pltpu.roll(sums, lax.rem(SETS - flat * share, SETS), 1)
    set_out[...] = turned[:1, :share]

    for other in peers:
        hazard_copy(other, me).wait_send()
    for z, other in targets:
        set_row(z, other, flat).wait_send()
    for q in other_chips:
        pair_copy(q).wait_send()
        block_copy(q, chip).wait_send()
    pair_copy(chip).wait_send()


def finish(pathwise, sets, pathwise_out, sets_out):
    pathwise_out[...] = pathwise[...]
    sets_out[...] = sets[...]


def solution(mesh):
    n_path, n_tm = mesh.shape["path"], mesh.shape["tm"]
    n_all = n_path * n_tm

    def on_device(values, hazard, spread, trade_set):
        paths, dates, trades = values.shape
        own = paths // n_tm
        chunks = paths // CHUNK_PATHS
        f32 = jnp.float32
        any_space = pl.BlockSpec(memory_space=pltpu.HBM)
        vmem = pl.BlockSpec(memory_space=pltpu.VMEM)
        dma = pltpu.SemaphoreType.DMA
        pathwise, sets = pl.pallas_call(
            functools.partial(kernel, n_path, n_tm),
            out_shape=(
                jax.ShapeDtypeStruct((own, SETS), f32),
                jax.ShapeDtypeStruct((1, SETS // n_all), f32),
            ),
            in_specs=[any_space, any_space, pl.BlockSpec(memory_space=pltpu.SMEM), any_space],
            out_specs=(vmem, vmem),
            scratch_shapes=[
                pltpu.VMEM((paths * dates, trades), jnp.bfloat16),
                pltpu.VMEM((trades // LANES, LANES), jnp.int32),
                pltpu.VMEM((SETS, trades), jnp.bfloat16),
                pltpu.VMEM((dates, paths), f32),
                pltpu.VMEM((chunks, SETS // LANES, CHUNK_PATHS * dates, LANES), f32),
                pltpu.VMEM((paths, 8), f32),
                pltpu.VMEM((paths, SETS), f32),
                pltpu.VMEM((n_tm // 2, own, SETS), f32),
                pltpu.VMEM((n_tm // 2, own, SETS), f32),
                pltpu.VMEM((n_tm // 2, own, SETS), f32),
                pltpu.VMEM((n_tm, dates, paths), f32),
                pltpu.VMEM((paths, 8), f32),
                pltpu.VMEM((n_tm, paths), f32),
                pltpu.VMEM((paths, n_tm), f32),
                pltpu.VMEM((1, SETS), f32),
                pltpu.VMEM((n_all, 1, SETS), f32),
                dma((chunks,)),
                dma((2,)),
                dma((n_tm,)),
                dma((n_tm,)),
                dma((n_tm // 2,)),
                dma((n_tm // 2,)),
                dma((n_tm // 2,)),
                dma((n_tm // 2,)),
                dma((n_all,)),
                dma((n_all,)),
                pltpu.SemaphoreType.REGULAR,
            ],
            compiler_params=pltpu.CompilerParams(
                collective_id=0, has_side_effects=True, vmem_limit_bytes=62 * 1024 * 1024
            ),
        )(values, hazard, spread, trade_set.reshape(trades // LANES, LANES))
        pathwise, sets = pl.pallas_call(
            finish,
            out_shape=(
                jax.ShapeDtypeStruct(pathwise.shape, f32),
                jax.ShapeDtypeStruct(sets.shape, f32),
            ),
            in_specs=[vmem, vmem],
            out_specs=(vmem, vmem),
        )(pathwise, sets)
        return pathwise, sets.reshape(SETS // n_all)

    in_specs = (P("path", "tm", None), P("tm", "path"), P("tm"), P())
    out_specs = (P(("path", "tm"), None), P(("path", "tm")))
    return jax.shard_map(
        on_device, mesh=mesh, in_specs=in_specs, out_specs=out_specs, check_vma=False
    )
```

profile of v0, /device:TPU:0, one launch (start us, length us, event | category | flops | bytes accessed | tf_op | source)
XLA Modules:
  0.0 18.3 jit_solution(12172590421992659482)
XLA Ops:
  0.6 16.2 %shard_map.59 = (f32[64,256]{1,0:T(8,128)}, f32[1,8]{1,0:T(1,128)}) custom-call(bf16[512,2,2048]{2,1,0:T(2,128)(2,1)} %values.1, f32[2,512]{1,0:T(2,128)} %hazard_in.1, f32[2]{0:T(128)} %spread.1, s32[16,128]{1,0:T(8,128)} %bitcast.2), custom_call_target="tpu_custom_call" | custom-call | tf_op jit(solution)/shard_map/pallas_call | solution.py:221
  16.8 1.5 %shard_map.60 = (f32[64,256]{1,0:T(8,128)}, f32[1,8]{1,0:T(1,128)}) custom-call(f32[64,256]{1,0:T(8,128)} %get-tuple-element.6.pathwise, f32[1,8]{1,0:T(1,128)} %get-tuple-element.7.sets), custom_call_target="tpu_custom_call" | custom-call | tf_op jit(solution)/shard_map/pallas_call | solution.py:262
where the time goes:
time: 18.5 us; the launch traced here: 18.3 us
  Pallas kernels  17.6 us (95%)
  between operations  0.64 us (3%)
    pallas_call x1, Pallas kernels, on_device(): pl.pallas_call(functools.partial(kernel, n_path, n_tm), out_shape=(jax.Sh...  16.2 us
    pallas_call x1, Pallas kernels, on_device(): pl.pallas_call(finish, out_shape=(jax.ShapeDtypeStruct(pathwise.shape, f3...  1.48 us

commit v1 on v0

v1 whole, which is shorter than its diff:
```python
import functools

import jax
import jax.numpy as jnp
from jax import lax
from jax.experimental import pallas as pl
from jax.experimental.pallas import tpu as pltpu
from jax.sharding import PartitionSpec as P

SETS = 256
CHUNK_PATHS = 128
LANES = 128
PACK = 16
BARRIER_AFTER = 0
MESH = pl.DeviceIdType.MESH
DOT_NT = (((1,), (1,)), ((), ()))


def kernel(
    n_path, n_tm, values, hazard_in, spread_in, trade_in, out, set_out,
    vbuf, ts, oh, hz, spread, nbuf, wt, contrib, pair, comb, recv, bsum, hbuf, pcol, ecol, row_a, rows_a,
    load_sem, small_sem, h_send, hp_recv, h_recv, p_send, p_recv, b_send, b_recv, a_send, a_recv, ready,
):
    paths, dates, trades = values.shape
    f32, bf16 = jnp.float32, jnp.bfloat16
    own = paths // n_tm
    chunks = paths // CHUNK_PATHS
    per = n_tm // chunks
    n_all = n_path * n_tm
    chips = n_tm // 2
    share = SETS // n_all
    path_at, me = lax.axis_index("path"), lax.axis_index("tm")
    flat = path_at * n_tm + me
    chip, core = lax.div(me, 2), lax.rem(me, 2)
    partner = me + 1 - 2 * core
    peers = [lax.rem(me + k, n_tm) for k in range(1, n_tm)]
    path_peers = [lax.rem(path_at + k, n_path) for k in range(1, n_path)]
    rows = CHUNK_PATHS * dates
    my_chunk = lax.div(me, per)
    if chunks == 4:
        high, low = lax.div(my_chunk, 2), lax.rem(my_chunk, 2)
        first = [2 * (1 - high) + 1 - low, 2 * high + 1 - low, 2 * (1 - high) + low, my_chunk]
    else:
        first = [lax.rem(my_chunk + 1 + i, chunks) for i in range(chunks)]
    flat_values = values.reshape(paths * dates, trades)

    def load(i):
        span = pl.ds(pl.multiple_of(first[i] * rows, rows), rows)
        return pltpu.make_async_copy(flat_values.at[span], vbuf.at[span], load_sem.at[i])

    copy_trades = pltpu.make_async_copy(trade_in, ts, small_sem.at[0])
    copy_hazard = pltpu.make_async_copy(hazard_in, hz, small_sem.at[1])
    copy_spread = pltpu.make_async_copy(spread_in, spread, small_sem.at[2])
    copy_trades.start()
    copy_hazard.start()
    copy_spread.start()
    for i in range(chunks):
        load(i).start()

    barrier = pltpu.get_barrier_semaphore()
    for other in peers:
        pl.semaphore_signal(barrier, inc=1, device_id=(path_at, other), device_id_type=MESH)
    for other in path_peers:
        pl.semaphore_signal(barrier, inc=1, device_id=(other, me), device_id_type=MESH)

    def remote(src, dst, send, recv_at, device):
        return pltpu.make_async_remote_copy(
            src_ref=src, dst_ref=dst, send_sem=send, recv_sem=recv_at, device_id=device, device_id_type=MESH
        )

    def own_rows(index):
        return pl.ds(pl.multiple_of(index * own, own), own)

    def hazard_copy(other, arrival):
        return remote(bsum, hbuf.at[me], h_send, arrival, (path_at, other))

    def hazards(count, send, arrival):
        span = hbuf.at[pl.ds(0, count)]
        return remote(span, span, send, arrival, (path_at, partner))

    def pair_copy(q):
        theirs = contrib.at[own_rows(q * 2 + 1 - core)]
        return remote(theirs, pair.at[q], p_send, p_recv.at[q], (path_at, partner))

    def block_copy(q, slot):
        return remote(comb.at[q], recv.at[slot], b_send, b_recv.at[slot], (path_at, q * 2 + core))

    targets = [(z, other) for z in path_peers for other in [me] + peers]
    targets += [(path_at, other) for other in peers]

    def set_row(z, other):
        half = lax.div((z * n_tm + other) * share, LANES)
        return remote(row_a.at[half], rows_a.at[flat], a_send, a_recv, (z, other))

    copy_trades.wait()
    base = lax.broadcasted_iota(jnp.int32, (PACK, LANES), 0)
    set_at = [(base + PACK * r).astype(f32).astype(bf16) for r in range(SETS // PACK)]
    one, zero = jnp.ones((PACK, LANES), bf16), jnp.zeros((PACK, LANES), bf16)
    for block in range(trades // LANES):
        ids = jnp.broadcast_to(ts[pl.ds(block, 1), :], (PACK, LANES)).astype(f32).astype(bf16)
        for r in range(SETS // PACK):
            picked = jnp.where(ids == set_at[r], one, zero)
            oh[pl.ds(r * PACK, PACK), pl.ds(block * LANES, LANES)] = picked.astype(oh.dtype)

    copy_hazard.wait()
    copy_spread.wait()
    total = jnp.zeros((1, paths), f32)
    weight_rows = []
    scale = 1.0 / (dates * n_tm)
    for d in range(dates):
        total = total + hz[pl.ds(d, 1), :]
        weight_rows.append((spread[d] * scale) * jnp.exp(-total))
    weight_rows.append(jnp.zeros((8 - dates, paths), f32))
    wt[...] = jnp.transpose(jnp.concatenate(weight_rows, axis=0))
    bsum[...] = total
    hbuf[me] = total

    def meet():
        pl.semaphore_wait(barrier, n_tm - 1 + n_path - 1)
        hazard_copy(partner, hp_recv).start()
        for other in peers:
            @pl.when(other != partner)
            def _():
                hazard_copy(other, h_recv).start()
        for other in path_peers:
            pl.semaphore_signal(ready, inc=1, device_id=(other, me), device_id_type=MESH)

    def exchange(i):
        for k in range(per // 2):
            pair_copy(first[i] * (per // 2) + k).start()

    def combine(q):
        remote(pair.at[q], pair.at[q], p_send, p_recv.at[q], (path_at, partner)).wait_recv()
        mine = own_rows(q * 2 + core)
        factor = pcol[mine, :]
        return factor[:, 0:1] * contrib[mine, :] + factor[:, 1:2] * pair[q]

    def forward(i):
        for k in range(per // 2):
            q = first[i] * (per // 2) + k
            comb[q] = combine(q)
            block_copy(q, chip).start()

    if BARRIER_AFTER < 0:
        meet()
    for i in range(chunks):
        load(i).wait()
        half_rows = rows // 2
        for k in range(2):
            begin = pl.multiple_of(first[i] * rows + k * half_rows, half_rows)
            netted = lax.dot_general(
                vbuf[pl.ds(begin, half_rows), :], oh[...], DOT_NT, preferred_element_type=f32
            )
            for h in range(SETS // LANES):
                nbuf[i, h, pl.ds(k * half_rows, half_rows)] = netted[:, h * LANES : (h + 1) * LANES]
        path_span = pl.ds(pl.multiple_of(first[i] * CHUNK_PATHS, CHUNK_PATHS), CHUNK_PATHS)
        weight = wt[path_span, :]
        for h in range(SETS // LANES):
            part = None
            for d in range(dates):
                picked = nbuf[i, h, pl.ds(d, CHUNK_PATHS, stride=dates), :]
                term = weight[:, d : d + 1] * jnp.maximum(picked, 0.0)
                part = term if part is None else part + term
            contrib[path_span, pl.ds(h * LANES, LANES)] = part
        if i == BARRIER_AFTER:
            meet()
        if i >= BARRIER_AFTER:
            for j in range(i + 1 if i == BARRIER_AFTER else 1):
                exchange(i if i != BARRIER_AFTER else j)

    hazards(1, h_send, hp_recv).wait_recv()
    block = hbuf[me - core]
    late = core.astype(f32)
    factors = [jnp.exp(-late * block), jnp.exp((late - 1.0) * block)]
    factors.append(jnp.zeros((6, paths), f32))
    pcol[...] = jnp.transpose(jnp.concatenate(factors, axis=0))
    for i in range(chunks - 2):
        forward(i)

    hazards(n_tm - 2, h_send, h_recv).wait_recv()
    before = jnp.zeros((1, paths), f32)
    for k in range(n_tm - 1):
        before = before + jnp.where(k < me, hbuf[k], 0.0)
    column = jnp.transpose(jnp.broadcast_to(jnp.exp(-before), (8, paths)))[:, 0:1]
    factor = jnp.broadcast_to(column, (paths, LANES))
    for h in range(SETS // LANES):
        part = jnp.sum(factor * contrib[:, pl.ds(h * LANES, LANES)], axis=0, keepdims=True)
        row_a[h] = part * (1.0 / (paths * n_path))
    pl.semaphore_wait(ready, n_path - 1)
    for z, other in targets:
        set_row(z, other).start()
    forward(chunks - 2)
    own_chips = [my_chunk * (per // 2) + lax.rem(lax.rem(chip, per // 2) + k, per // 2) for k in range(per // 2)]
    for q in own_chips[1:]:
        comb[q] = combine(q)
        block_copy(q, chip).start()
    my_half = lax.div(flat * share, LANES)
    rows_a[flat] = row_a[my_half]
    before = jnp.zeros((1, paths), f32)
    prefix = []
    for k in range(n_tm):
        prefix.append(before)
        before = before + hbuf[k]
    ecol[...] = jnp.transpose(jnp.exp(-jnp.concatenate(prefix, axis=0)))
    factor = ecol[own_rows(me), :]
    recv[chip] = combine(own_chips[0])

    other_chips = [lax.rem(chip + k, chips) for k in range(1, chips)]
    for q in other_chips:
        remote(recv.at[q], recv.at[q], b_send, b_recv.at[q], (path_at, me)).wait_recv()
    result = None
    for k in range(chips):
        term = factor[:, 2 * k : 2 * k + 1] * recv[k]
        result = term if result is None else result + term
    out[...] = result

    span = rows_a.at[pl.ds(0, n_all - 1)]
    arrived = remote(span, span, a_send, a_recv, (path_at, partner))
    arrived.wait_recv()
    sums = jnp.broadcast_to(jnp.sum(rows_a[...], axis=0), (8, LANES))
    turned = pltpu.roll(sums, lax.rem(LANES - (flat * share - my_half * LANES), LANES), 1)
    set_out[...] = turned[:1, :share]

    arrived.wait_send()
    hazards(n_tm - 1, h_send, h_recv).wait_send()
    span = recv.at[pl.ds(0, chips - 1)]
    remote(span, span, b_send, b_recv.at[0], (path_at, partner)).wait_send()
    remote(pair, pair, p_send, p_recv.at[0], (path_at, partner)).wait_send()


def finish(pathwise, sets, pathwise_out, sets_out, sem):
    copies = [
        pltpu.make_async_copy(pathwise, pathwise_out, sem.at[0]),
        pltpu.make_async_copy(sets, sets_out, sem.at[1]),
    ]
    for copy in copies:
        copy.start()
    for copy in copies:
        copy.wait()


def solution(mesh):
    n_path, n_tm = mesh.shape["path"], mesh.shape["tm"]
    n_all = n_path * n_tm

    def on_device(values, hazard, spread, trade_set):
        paths, dates, trades = values.shape
        own = paths // n_tm
        chunks = paths // CHUNK_PATHS
        f32 = jnp.float32
        hbm = pl.BlockSpec(memory_space=pltpu.HBM)
        vmem = pl.BlockSpec(memory_space=pltpu.VMEM)
        dma = pltpu.SemaphoreType.DMA
        pathwise, sets = pl.pallas_call(
            functools.partial(kernel, n_path, n_tm),
            out_shape=(pltpu.VMEM((own, SETS), f32), pltpu.VMEM((1, SETS // n_all), f32)),
            in_specs=[hbm, hbm, hbm, hbm],
            out_specs=(vmem, vmem),
            scratch_shapes=[
                pltpu.VMEM((paths * dates, trades), jnp.bfloat16),
                pltpu.VMEM((trades // LANES, LANES), jnp.int32),
                pltpu.VMEM((SETS, trades), jnp.float8_e4m3fn),
                pltpu.VMEM((dates, paths), f32),
                pltpu.SMEM((dates,), f32),
                pltpu.VMEM((chunks, SETS // LANES, CHUNK_PATHS * dates, LANES), f32),
                pltpu.VMEM((paths, 8), f32),
                pltpu.VMEM((paths, SETS), f32),
                pltpu.VMEM((n_tm // 2, own, SETS), f32),
                pltpu.VMEM((n_tm // 2, own, SETS), f32),
                pltpu.VMEM((n_tm // 2, own, SETS), f32),
                pltpu.VMEM((1, paths), f32),
                pltpu.VMEM((n_tm, 1, paths), f32),
                pltpu.VMEM((paths, 8), f32),
                pltpu.VMEM((paths, n_tm), f32),
                pltpu.VMEM((SETS // LANES, 1, LANES), f32),
                pltpu.VMEM((n_all, 1, LANES), f32),
                dma((chunks,)),
                dma((3,)),
                dma,
                dma,
                dma,
                dma,
                dma((n_tm // 2,)),
                dma,
                dma((n_tm // 2,)),
                dma,
                dma,
                pltpu.SemaphoreType.REGULAR,
            ],
            compiler_params=pltpu.CompilerParams(
                collective_id=0, has_side_effects=True, vmem_limit_bytes=62 * 1024 * 1024
            ),
        )(values, hazard, spread, trade_set.reshape(trades // LANES, LANES))
        pathwise = pltpu.with_memory_space_constraint(pathwise, pltpu.VMEM)
        sets = pltpu.with_memory_space_constraint(sets, pltpu.VMEM)
        pathwise, sets = pl.pallas_call(
            finish,
            out_shape=(
                jax.ShapeDtypeStruct(pathwise.shape, f32),
                jax.ShapeDtypeStruct(sets.shape, f32),
            ),
            in_specs=[vmem, vmem],
            out_specs=(hbm, hbm),
            scratch_shapes=[dma((2,))],
        )(pathwise, sets)
        return pathwise, sets.reshape(SETS // n_all)

    in_specs = (P("path", "tm", None), P("tm", "path"), P("tm"), P())
    out_specs = (P(("path", "tm"), None), P(("path", "tm")))
    return jax.shard_map(
        on_device, mesh=mesh, in_specs=in_specs, out_specs=out_specs, check_vma=False
    )
```

time: 18.5 us -> 15.2 us (0.82)
  Pallas kernels: 17.6 us -> 14.4 us
    pallas_call x1, Pallas kernels: 16.2 us -> 13.7 us  [on_device(): pl.pallas_call(functools.partial(kernel, n_path, n_tm), out_shape=(pltpu....]
    pallas_call x1, Pallas kernels: 1.48 us -> 0.65 us  [on_device(): pl.pallas_call(finish, out_shape=(jax.ShapeDtypeStruct(pathwise.shape, f3...]
where the time goes in v1:
time: 15.2 us; the launch traced here: 15 us
  Pallas kernels  14.4 us (95%)
  between operations  0.64 us (4%)
    pallas_call x1, Pallas kernels, on_device(): pl.pallas_call(functools.partial(kernel, n_path, n_tm), out_shape=(pltpu....  13.7 us
    pallas_call x1, Pallas kernels, on_device(): pl.pallas_call(finish, out_shape=(jax.ShapeDtypeStruct(pathwise.shape, f3...  0.65 us

profile of v1, /device:TPU:0, one launch (start us, length us, event | category | flops | bytes accessed | tf_op | source)
XLA Modules:
  0.0 15.0 jit_solution(176501576538016458)
XLA Ops:
  0.6 13.7 %shard_map.59 = (f32[64,256]{1,0:T(8,128)S(1)}, f32[1,8]{1,0:T(1,128)S(1)}) custom-call(bf16[512,2,2048]{2,1,0:T(2,128)(2,1)} %values.1, f32[2,512]{1,0:T(2,128)} %hazard_in.1, f32[2]{0:T(128)} %spread_in.1, s32[16,128]{1,0:T(8,128)} %bitcast.2), custom_call_target="tpu_custom_call" | custom-call | tf_op jit(solution)/shard_map/pallas_call | solution.py:254
  14.4 0.7 %shard_map.60 = (f32[64,256]{1,0:T(8,128)}, f32[1,8]{1,0:T(1,128)}) custom-call(f32[64,256]{1,0:T(8,128)S(1)} %get-tuple-element.6.pathwise, f32[1,8]{1,0:T(1,128)S(1)} %get-tuple-element.7.sets), custom_call_target="tpu_custom_call" | custom-call | tf_op jit(solution)/shard_map/pallas_call | solution.py:296

commit v2 on v1

v2 whole, which is shorter than its diff:
```python
import functools

import jax
import jax.numpy as jnp
from jax import lax
from jax.experimental import pallas as pl
from jax.experimental.pallas import tpu as pltpu
from jax.sharding import PartitionSpec as P

SETS = 256
CHUNK_PATHS = 128
LANES = 128
PACK = 16
TILE = 256
BARRIER_AFTER = 0
MESH = pl.DeviceIdType.MESH


def kernel(n_path, n_tm, *refs):
    rows = CHUNK_PATHS * refs[0].shape[1]
    sums = [pltpu.ACC(unit)((rows, SETS), jnp.float32) for unit in (0, 0, 1, 1)]
    sums += [pltpu.ACC(unit)((PACK, SETS), jnp.float32) for unit in (0, 1)]
    pl.run_scoped(lambda *totals: body(n_path, n_tm, totals, *refs), *sums)


def body(
    n_path, n_tm, totals, values, hazard_in, spread_in, trade_in, out, set_out,
    vbuf, ts, oh, hz, spread, nbuf, wt, contrib, theirs, comb, recv, bsum, before_me, hbuf, pcol, ecol, limbs, row_a, rows_a,
    load_sem, small_sem, h_send, h_recv, p_send, p_recv, b_send, b_recv, a_send, a_recv, ready, above,
):
    paths, dates, trades = values.shape
    f32, bf16 = jnp.float32, jnp.bfloat16
    own = paths // n_tm
    chunks = paths // CHUNK_PATHS
    per = n_tm // chunks
    n_all = n_path * n_tm
    chips = n_tm // 2
    share = SETS // n_all
    path_at, me = lax.axis_index("path"), lax.axis_index("tm")
    flat = path_at * n_tm + me
    chip, core = lax.div(me, 2), lax.rem(me, 2)
    partner = me + 1 - 2 * core
    peers = [lax.rem(me + k, n_tm) for k in range(1, n_tm)]
    leads = core == 1
    senders = n_path * chips
    slot = path_at * chips + chip
    rows = CHUNK_PATHS * dates
    my_chunk = lax.div(me, per)
    if chunks == 4:
        high, low = lax.div(my_chunk, 2), lax.rem(my_chunk, 2)
        first = [2 * (1 - high) + 1 - low, 2 * high + 1 - low, 2 * (1 - high) + low, my_chunk]
    else:
        first = [lax.rem(my_chunk + 1 + i, chunks) for i in range(chunks)]
    flat_values = values.reshape(paths * dates, trades)

    def load(i):
        span = pl.ds(pl.multiple_of(first[i] * rows, rows), rows)
        return pltpu.make_async_copy(flat_values.at[span], vbuf.at[span], load_sem.at[i])

    barrier = pltpu.get_barrier_semaphore()
    for other in peers:
        pl.semaphore_signal(barrier, inc=1, device_id=(path_at, other), device_id_type=MESH)

    copy_trades = pltpu.make_async_copy(trade_in, ts, small_sem.at[0])
    copy_hazard = pltpu.make_async_copy(hazard_in, hz, small_sem.at[1])
    copy_spread = pltpu.make_async_copy(spread_in, spread, small_sem.at[2])
    copy_trades.start()
    copy_hazard.start()
    copy_spread.start()
    for i in range(chunks):
        load(i).start()
    for z in range(1, n_path):
        @pl.when(z > path_at)
        def _():
            pl.semaphore_signal(barrier, inc=1, device_id=(z, me), device_id_type=MESH)

    def remote(src, dst, send, recv_at, device):
        return pltpu.make_async_remote_copy(
            src_ref=src, dst_ref=dst, send_sem=send, recv_sem=recv_at, device_id=device, device_id_type=MESH
        )

    def chunk_span(i):
        return pl.ds(pl.multiple_of(first[i] * CHUNK_PATHS, CHUNK_PATHS), CHUNK_PATHS)

    def own_rows(index):
        return pl.ds(pl.multiple_of(index * own, own), own)

    def hazard_copy(other, arrival):
        return remote(bsum, hbuf.at[me], h_send, h_recv.at[arrival], (path_at, other))

    def hazards(count, arrival):
        span = hbuf.at[pl.ds(0, count)]
        return remote(span, span, h_send, h_recv.at[arrival], (path_at, partner))

    def from_chips(arrival, chips_there):
        for c in range(1, chips):
            @pl.when(chips_there == c)
            def _():
                hazards(2 * c, arrival).wait_recv()

    def both_rows(q):
        return pl.ds(pl.multiple_of(q * 2 * own, 2 * own), 2 * own)

    def pair_copy(q, span):
        return remote(contrib.at[span], theirs.at[span], p_send, p_recv.at[q], (path_at, partner))

    def per_core(q, act):
        @pl.when(leads)
        def _():
            act(q, own_rows(q * 2), both_rows(q))

        @pl.when(jnp.logical_not(leads))
        def _():
            act(q, both_rows(q), own_rows(q * 2))

    def block_copy(q, slot_at):
        return remote(comb.at[own_rows(q * 2 + core)], recv.at[slot_at], b_send, b_recv, (path_at, q * 2 + core))

    def set_row(z, other):
        half = lax.div((z * n_tm + other) * share, LANES)
        return remote(row_a.at[half], rows_a.at[slot], a_send, a_recv, (z, other))

    def set_rows(count):
        span = rows_a.at[pl.ds(0, count)]
        return remote(span, span, a_send, a_recv, (path_at, partner))

    copy_trades.wait()
    base = lax.broadcasted_iota(jnp.int32, (PACK, LANES), 0)
    set_at = [(base + PACK * r).astype(f32).astype(bf16) for r in range(SETS // PACK)]
    one, zero = jnp.ones((PACK, LANES), bf16), jnp.zeros((PACK, LANES), bf16)
    for block in range(trades // LANES):
        ids = jnp.broadcast_to(ts[pl.ds(block, 1), :], (PACK, LANES)).astype(f32).astype(bf16)
        for r in range(SETS // PACK):
            picked = jnp.where(ids == set_at[r], one, zero)
            oh[pl.ds(r * PACK, PACK), pl.ds(block * LANES, LANES)] = picked.astype(oh.dtype)

    copy_hazard.wait()
    copy_spread.wait()
    total = jnp.zeros((1, paths), f32)
    weight_rows = []
    scale = 1.0 / (dates * n_tm)
    for d in range(dates):
        total = total + hz[pl.ds(d, 1), :]
        weight_rows.append((spread[d] * scale) * jnp.exp(-total))
    weight_rows.append(jnp.zeros((8 - dates, paths), f32))
    wt[...] = jnp.transpose(jnp.concatenate(weight_rows, axis=0))
    bsum[...] = total
    hbuf[me] = total

    def meet():
        pl.semaphore_wait(barrier, n_tm - 1 + path_at)
        hazard_copy(partner, 0).start()
        for side in (1, 0):
            for k in range(1, chips):
                there = lax.rem(chip + k, chips)
                hazard_copy(there * 2 + side, jnp.where(there > chip, 1, 2)).start()
        for k in range(chips):
            @pl.when(jnp.logical_or(jnp.logical_not(leads), k > 0))
            def _():
                other = lax.rem(chip + k, chips) * 2 + 1
                pl.semaphore_signal(ready, inc=1, device_id=(path_at, other), device_id_type=MESH)
        for z in range(n_path - 1):
            @pl.when(jnp.logical_and(leads, z < path_at))
            def _():
                pl.semaphore_signal(above, inc=1, device_id=(z, me), device_id_type=MESH)

    def exchange(i):
        for k in range(per // 2):
            per_core(first[i] * (per // 2) + k, lambda q, send, take: pair_copy(q, send).start())

    def combine(q):
        per_core(q, lambda q, send, take: pair_copy(q, take).wait_recv())

        @pl.when(leads)
        def _():
            span = both_rows(q)
            both = theirs[span, :] + pcol[span, 0:1] * contrib[span, :]
            comb[span, :] = both
            upper = both.astype(bf16)
            limbs[0, span, :] = upper
            limbs[1, span, :] = (both - upper.astype(f32)).astype(bf16)

        @pl.when(jnp.logical_not(leads))
        def _():
            span = own_rows(q * 2)
            comb[span, :] = contrib[span, :] + pcol[span, 0:1] * theirs[span, :]

    own_chips = [my_chunk * (per // 2) + lax.rem(lax.rem(chip, per // 2) + k, per // 2) for k in range(per // 2)]
    other_chips = [first[i] * (per // 2) + k for i in range(chunks - 1) for k in range(per // 2)]
    other_chips += own_chips[1:]

    tiles = trades // TILE // 2

    def multiply(i):
        span = pl.ds(pl.multiple_of(first[i] * rows, rows), rows)
        for t in range(tiles):
            for unit in range(2):
                ids = oh[:, pl.ds((unit * tiles + t) * TILE, TILE)]
                pltpu.matmul_push_rhs(ids, staging_register=t % 2, mxu_index=unit, transpose=True)
            for unit in range(2):
                block = vbuf[span, pl.ds((unit * tiles + t) * TILE, TILE)]
                pltpu.matmul_acc_lhs(totals[unit * 2 + i % 2], block, load_staged_rhs=t % 2)

    def weigh(i):
        netted = pltpu.matmul_pop(totals[i % 2]) + pltpu.matmul_pop(totals[2 + i % 2])
        for h in range(SETS // LANES):
            nbuf[i, h] = netted[:, h * LANES : (h + 1) * LANES]
        path_span = chunk_span(i)
        weight = wt[path_span, :]
        for h in range(SETS // LANES):
            part = None
            for d in range(dates):
                picked = nbuf[i, h, pl.ds(d, CHUNK_PATHS, stride=dates), :]
                term = weight[:, d : d + 1] * jnp.maximum(picked, 0.0)
                part = term if part is None else part + term
            contrib[path_span, pl.ds(h * LANES, LANES)] = part

    if BARRIER_AFTER < 0:
        meet()
    for i in range(chunks):
        load(i).wait()
        if i > 0:
            weigh(i - 1)
        multiply(i)
        if i == BARRIER_AFTER:
            meet()
        if i > 0 and i >= BARRIER_AFTER:
            for j in range(0 if i == BARRIER_AFTER else i - 1, i):
                exchange(j)
    weigh(chunks - 1)
    exchange(chunks - 1)

    @pl.when(leads)
    def _():
        hazards(1, 0).wait_recv()
    block = jnp.broadcast_to(jnp.exp(-hbuf[me - core]), (8, paths))
    pcol[...] = jnp.transpose(block)
    for q in other_chips:
        combine(q)

        @pl.when(jnp.logical_not(leads))
        def _():
            block_copy(q, chip).start()

    combine(own_chips[0])

    def limb(unit, t, part):
        block = limbs[part, pl.ds((unit * row_tiles + t) * TILE, TILE), :]
        pltpu.matmul_push_rhs(block, staging_register=part, mxu_index=unit)

    row_tiles = paths // TILE // 2
    @pl.when(leads)
    def _():
        for unit in range(2):
            for part in range(2):
                limb(unit, 0, part)
        from_chips(1, chip)
        before_me[...] = jnp.zeros((1, paths), f32)
        for c in range(1, chips):
            @pl.when(chip == c)
            def _():
                before_me[...] = sum(hbuf[k] for k in range(2 * c))
        earlier = jnp.broadcast_to(jnp.exp(-before_me[...]), (PACK, paths))
        upper = earlier.astype(bf16).astype(f32)
        at = lax.broadcasted_iota(jnp.int32, (PACK, paths), 0)
        weights = jnp.where(at == 0, upper, jnp.where(at == 1, earlier - upper, 0.0)).astype(bf16)
        for t in range(row_tiles):
            for unit in range(2):
                if t > 0:
                    limb(unit, t, 0)
                    limb(unit, t, 1)
                begin = (unit * row_tiles + t) * TILE
                for part in range(2):
                    pltpu.matmul_acc_lhs(totals[4 + unit], weights[:, begin : begin + TILE], load_staged_rhs=part)
        both = pltpu.matmul_pop(totals[4]) + pltpu.matmul_pop(totals[5])
        line = (both[0:1] + both[1:2]) * (1.0 / (paths * n_path))
        for h in range(SETS // LANES):
            row_a[h] = line[:, h * LANES : (h + 1) * LANES]
        pl.semaphore_wait(ready, n_tm - 1)
        for z in range(n_path - 1):
            @pl.when(z < path_at)
            def _():
                for k in range(n_tm):
                    set_row(z, lax.rem(me + 1 + k, n_tm)).start()
        for other in peers:
            set_row(path_at, other).start()

        @pl.when(path_at < n_path - 1)
        def _():
            pl.semaphore_wait(above, n_path - 1 - path_at)
        for z in range(1, n_path):
            @pl.when(z > path_at)
            def _():
                for k in range(n_tm):
                    set_row(z, lax.rem(me + 1 + k, n_tm)).start()
        for q in other_chips:
            block_copy(q, chip).start()
        rows_a[slot] = row_a[lax.div(flat * share, LANES)]

    from_chips(2, chips - 1 - chip)

    @pl.when(jnp.logical_not(leads))
    def _():
        hazards(1, 0).wait_recv()
        from_chips(1, chip)
    before = jnp.zeros((1, paths), f32)
    prefix = []
    for k in range(n_tm):
        if k % 2 == 0:
            prefix.append(before)
        before = before + hbuf[k]
    if chips < 8:
        prefix.append(jnp.zeros((8 - chips, paths), f32))
    ecol[...] = jnp.transpose(jnp.exp(-jnp.concatenate(prefix, axis=0)))
    factor = ecol[own_rows(me), :]
    recv[chip] = comb[own_rows(me), :]

    span = recv.at[pl.ds(0, chips - 1)]
    blocks = remote(span, span, b_send, b_recv, (path_at, partner))
    blocks.wait_recv()
    result = None
    for k in range(chips):
        term = factor[:, k : k + 1] * recv[k]
        result = term if result is None else result + term
    out[...] = result

    @pl.when(leads)
    def _():
        set_rows(senders - 1).wait_recv()

    @pl.when(jnp.logical_not(leads))
    def _():
        set_rows(senders).wait_recv()
    sums = jnp.broadcast_to(jnp.sum(rows_a[...], axis=0), (8, LANES))
    turned = pltpu.roll(sums, lax.rem(LANES - lax.rem(flat * share, LANES), LANES), 1)
    set_out[...] = turned[:1, :share]

    span = hbuf.at[pl.ds(0, n_tm - 1)]
    remote(span, span, h_send, h_recv.at[0], (path_at, partner)).wait_send()
    blocks.wait_send()

    @pl.when(leads)
    def _():
        span = rows_a.at[pl.ds(0, senders - 1)]
        sent = remote(span, span, a_send, a_recv, (path_at, partner))
        sent.wait_send()
        span = rows_a.at[pl.ds(0, senders)]
        sent = remote(span, span, a_send, a_recv, (path_at, partner))
        sent.wait_send()
        span = theirs.at[pl.ds(0, paths // 2)]
        remote(span, span, p_send, p_recv.at[0], (path_at, partner)).wait_send()

    @pl.when(jnp.logical_not(leads))
    def _():
        remote(theirs, theirs, p_send, p_recv.at[0], (path_at, partner)).wait_send()


def finish(pathwise, sets, pathwise_out, sets_out, sem):
    copies = [
        pltpu.make_async_copy(pathwise, pathwise_out, sem.at[0]),
        pltpu.make_async_copy(sets, sets_out, sem.at[1]),
    ]
    for copy in copies:
        copy.start()
    for copy in copies:
        copy.wait()


def solution(mesh):
    n_path, n_tm = mesh.shape["path"], mesh.shape["tm"]
    n_all = n_path * n_tm

    def on_device(values, hazard, spread, trade_set):
        paths, dates, trades = values.shape
        own = paths // n_tm
        chunks = paths // CHUNK_PATHS
        f32 = jnp.float32
        hbm = pl.BlockSpec(memory_space=pltpu.HBM)
        vmem = pl.BlockSpec(memory_space=pltpu.VMEM)
        dma = pltpu.SemaphoreType.DMA
        pathwise, sets = pl.pallas_call(
            functools.partial(kernel, n_path, n_tm),
            out_shape=(pltpu.VMEM((own, SETS), f32), pltpu.VMEM((1, SETS // n_all), f32)),
            in_specs=[hbm, hbm, hbm, hbm],
            out_specs=(vmem, vmem),
            scratch_shapes=[
                pltpu.VMEM((paths * dates, trades), jnp.bfloat16),
                pltpu.VMEM((trades // LANES, LANES), jnp.int32),
                pltpu.VMEM((SETS, trades), jnp.float8_e4m3fn),
                pltpu.VMEM((dates, paths), f32),
                pltpu.SMEM((dates,), f32),
                pltpu.VMEM((chunks, SETS // LANES, CHUNK_PATHS * dates, LANES), f32),
                pltpu.VMEM((paths, 8), f32),
                pltpu.VMEM((paths, SETS), f32),
                pltpu.VMEM((paths, SETS), f32),
                pltpu.VMEM((paths, SETS), f32),
                pltpu.VMEM((n_tm // 2, own, SETS), f32),
                pltpu.VMEM((1, paths), f32),
                pltpu.VMEM((1, paths), f32),
                pltpu.VMEM((n_tm, 1, paths), f32),
                pltpu.VMEM((paths, 8), f32),
                pltpu.VMEM((paths, max(8, n_tm // 2)), f32),
                pltpu.VMEM((2, paths, SETS), jnp.bfloat16),
                pltpu.VMEM((SETS // LANES, 1, LANES), f32),
                pltpu.VMEM((n_all // 2, 1, LANES), f32),
                dma((chunks,)),
                dma((3,)),
                dma,
                dma((3,)),
                dma,
                dma((n_tm // 2,)),
                dma,
                dma,
                dma,
                dma,
                pltpu.SemaphoreType.REGULAR,
                pltpu.SemaphoreType.REGULAR,
            ],
            compiler_params=pltpu.CompilerParams(
                collective_id=0, has_side_effects=True, vmem_limit_bytes=62 * 1024 * 1024
            ),
        )(values, hazard, spread, trade_set.reshape(trades // LANES, LANES))
        pathwise = pltpu.with_memory_space_constraint(pathwise, pltpu.VMEM)
        sets = pltpu.with_memory_space_constraint(sets, pltpu.VMEM)
        pathwise, sets = pl.pallas_call(
            finish,
            out_shape=(
                jax.ShapeDtypeStruct(pathwise.shape, f32),
                jax.ShapeDtypeStruct(sets.shape, f32),
            ),
            in_specs=[vmem, vmem],
            out_specs=(hbm, hbm),
            scratch_shapes=[dma((2,))],
        )(pathwise, sets)
        return pathwise, sets.reshape(SETS // n_all)

    in_specs = (P("path", "tm", None), P("tm", "path"), P("tm"), P())
    out_specs = (P(("path", "tm"), None), P(("path", "tm")))
    return jax.shard_map(
        on_device, mesh=mesh, in_specs=in_specs, out_specs=out_specs, check_vma=False
    )
```

time: 15.2 us -> 14.1 us (0.928)
  Pallas kernels: 14.4 us -> 13.3 us
    pallas_call x1, Pallas kernels: 13.7 us -> 12.6 us  [on_device(): pl.pallas_call(functools.partial(kernel, n_path, n_tm), out_shape=(pltpu....]
where the time goes in v2:
time: 14.1 us; the launch traced here: 13.9 us
  Pallas kernels  13.3 us (94%)
  between operations  0.64 us (5%)
    pallas_call x1, Pallas kernels, on_device(): pl.pallas_call(functools.partial(kernel, n_path, n_tm), out_shape=(pltpu....  12.6 us
    pallas_call x1, Pallas kernels, on_device(): pl.pallas_call(finish, out_shape=(jax.ShapeDtypeStruct(pathwise.shape, f3...  0.65 us

profile of v2, /device:TPU:0, one launch (start us, length us, event | category | flops | bytes accessed | tf_op | source)
XLA Modules:
  0.0 13.9 jit_solution(864860546841526897)
XLA Ops:
  0.6 12.6 %shard_map.59 = (f32[64,256]{1,0:T(8,128)S(1)}, f32[1,8]{1,0:T(1,128)S(1)}) custom-call(bf16[512,2,2048]{2,1,0:T(2,128)(2,1)} %refs_0_.1, f32[2,512]{1,0:T(2,128)} %refs_1_.1, f32[2]{0:T(128)} %refs_2_.1, s32[16,128]{1,0:T(8,128)} %bitcast.2), custom_call_target="tpu_custom_call" | custom-call | tf_op jit(solution)/shard_map/pallas_call | solution.py:381
  13.3 0.7 %shard_map.60 = (f32[64,256]{1,0:T(8,128)}, f32[1,8]{1,0:T(1,128)}) custom-call(f32[64,256]{1,0:T(8,128)S(1)} %get-tuple-element.6.pathwise, f32[1,8]{1,0:T(1,128)S(1)} %get-tuple-element.7.sets), custom_call_target="tpu_custom_call" | custom-call | tf_op jit(solution)/shard_map/pallas_call | solution.py:425

commit v3 on v2

--- a/solution.py
+++ b/solution.py
@@ -12,7 +12,7 @@
 LANES = 128
 PACK = 16
 TILE = 256
-BARRIER_AFTER = 0
+BARRIER_AFTER = 1
 MESH = pl.DeviceIdType.MESH
 
 
@@ -25,8 +25,8 @@
 
 def body(
     n_path, n_tm, totals, values, hazard_in, spread_in, trade_in, out, set_out,
-    vbuf, ts, oh, hz, spread, nbuf, wt, contrib, theirs, comb, recv, bsum, before_me, hbuf, pcol, ecol, limbs, row_a, rows_a,
-    load_sem, small_sem, h_send, h_recv, p_send, p_recv, b_send, b_recv, a_send, a_recv, ready, above,
+    vbuf, ts, oh, hz, spread, nbuf, wt, contrib, theirs, comb, recv, bsum, mate_sum, before_me, hbuf, pcol, ecol, limbs, row_a, rows_a,
+    load_sem, small_sem, h_send, h_recv, p_send, p_recv, b_send, b_recv, a_send, a_recv, mate, ready, above,
 ):
     paths, dates, trades = values.shape
     f32, bf16 = jnp.float32, jnp.bfloat16
@@ -42,6 +42,7 @@
     partner = me + 1 - 2 * core
     peers = [lax.rem(me + k, n_tm) for k in range(1, n_tm)]
     leads = core == 1
+    lead_peers = [lax.rem(chip + k, chips) * 2 + 1 for k in range(1, chips)]
     senders = n_path * chips
     slot = path_at * chips + chip
     rows = CHUNK_PATHS * dates
@@ -53,13 +54,24 @@
         first = [lax.rem(my_chunk + 1 + i, chunks) for i in range(chunks)]
     flat_values = values.reshape(paths * dates, trades)
 
-    def load(i):
+    half = trades // 2
+    halved = tuple(range(chunks))
+
+    def load(i, part):
         span = pl.ds(pl.multiple_of(first[i] * rows, rows), rows)
-        return pltpu.make_async_copy(flat_values.at[span], vbuf.at[span], load_sem.at[i])
+        at = i + sum(j < i for j in halved) + part
+        if i in halved:
+            area = (span, pl.ds(part * half, half))
+            return pltpu.make_async_copy(flat_values.at[area], vbuf.at[area], load_sem.at[at])
+        return pltpu.make_async_copy(flat_values.at[span], vbuf.at[span], load_sem.at[at])
 
     barrier = pltpu.get_barrier_semaphore()
-    for other in peers:
-        pl.semaphore_signal(barrier, inc=1, device_id=(path_at, other), device_id_type=MESH)
+    pl.semaphore_signal(barrier, inc=1, device_id=(path_at, partner), device_id_type=MESH)
+
+    @pl.when(leads)
+    def _():
+        for other in lead_peers:
+            pl.semaphore_signal(barrier, inc=1, device_id=(path_at, other), device_id_type=MESH)
 
     copy_trades = pltpu.make_async_copy(trade_in, ts, small_sem.at[0])
     copy_hazard = pltpu.make_async_copy(hazard_in, hz, small_sem.at[1])
@@ -68,7 +80,9 @@
     copy_hazard.start()
     copy_spread.start()
     for i in range(chunks):
-        load(i).start()
+        load(i, 0).start()
+        if i in halved:
+            load(i, 1).start()
     for z in range(1, n_path):
         @pl.when(z > path_at)
         def _():
@@ -85,8 +99,8 @@
     def own_rows(index):
         return pl.ds(pl.multiple_of(index * own, own), own)
 
-    def hazard_copy(other, arrival):
-        return remote(bsum, hbuf.at[me], h_send, h_recv.at[arrival], (path_at, other))
+    def row_copy(src, dst, arrival, other):
+        return remote(src, dst, h_send, h_recv.at[arrival], (path_at, other))
 
     def hazards(count, arrival):
         span = hbuf.at[pl.ds(0, count)]
@@ -96,7 +110,7 @@
         for c in range(1, chips):
             @pl.when(chips_there == c)
             def _():
-                hazards(2 * c, arrival).wait_recv()
+                hazards(c, arrival).wait_recv()
 
     def both_rows(q):
         return pl.ds(pl.multiple_of(q * 2 * own, 2 * own), 2 * own)
@@ -117,8 +131,8 @@
         return remote(comb.at[own_rows(q * 2 + core)], recv.at[slot_at], b_send, b_recv, (path_at, q * 2 + core))
 
     def set_row(z, other):
-        half = lax.div((z * n_tm + other) * share, LANES)
-        return remote(row_a.at[half], rows_a.at[slot], a_send, a_recv, (z, other))
+        piece = lax.div((z * n_tm + other) * share, LANES)
+        return remote(row_a.at[piece], rows_a.at[slot], a_send, a_recv, (z, other))
 
     def set_rows(count):
         span = rows_a.at[pl.ds(0, count)]
@@ -145,24 +159,25 @@
     weight_rows.append(jnp.zeros((8 - dates, paths), f32))
     wt[...] = jnp.transpose(jnp.concatenate(weight_rows, axis=0))
     bsum[...] = total
-    hbuf[me] = total
 
     def meet():
-        pl.semaphore_wait(barrier, n_tm - 1 + path_at)
-        hazard_copy(partner, 0).start()
-        for side in (1, 0):
+        pl.semaphore_wait(barrier, 1 + path_at + core * (chips - 1))
+
+        @pl.when(jnp.logical_not(leads))
+        def _():
+            row_copy(bsum, mate_sum, 0, partner).start()
+            pl.semaphore_signal(mate, inc=1, device_id=(path_at, partner), device_id_type=MESH)
+
+        @pl.when(leads)
+        def _():
+            pl.semaphore_wait(mate, 1)
+            for other in lead_peers:
+                pl.semaphore_signal(ready, inc=1, device_id=(path_at, other), device_id_type=MESH)
+            row_copy(bsum, mate_sum, 0, partner).wait_recv()
+            hbuf[chip] = bsum[...] + mate_sum[...]
             for k in range(1, chips):
                 there = lax.rem(chip + k, chips)
-                hazard_copy(there * 2 + side, jnp.where(there > chip, 1, 2)).start()
-        for k in range(chips):
-            @pl.when(jnp.logical_or(jnp.logical_not(leads), k > 0))
-            def _():
-                other = lax.rem(chip + k, chips) * 2 + 1
-                pl.semaphore_signal(ready, inc=1, device_id=(path_at, other), device_id_type=MESH)
-        for z in range(n_path - 1):
-            @pl.when(jnp.logical_and(leads, z < path_at))
-            def _():
-                pl.semaphore_signal(above, inc=1, device_id=(z, me), device_id_type=MESH)
+                row_copy(hbuf.at[chip], hbuf.at[chip], jnp.where(there > chip, 1, 2), there * 2 + 1).start()
 
     def exchange(i):
         for k in range(per // 2):
@@ -191,15 +206,20 @@
 
     tiles = trades // TILE // 2
 
-    def multiply(i):
+    def push(n):
+        for unit in range(2):
+            ids = oh[:, pl.ds((2 * (n % tiles) + unit) * TILE, TILE)]
+            pltpu.matmul_push_rhs(ids, staging_register=n % 2, mxu_index=unit, transpose=True)
+
+    def multiply(i, steps):
         span = pl.ds(pl.multiple_of(first[i] * rows, rows), rows)
-        for t in range(tiles):
+        for t in steps:
+            n = i * tiles + t
+            if n + 1 < chunks * tiles:
+                push(n + 1)
             for unit in range(2):
-                ids = oh[:, pl.ds((unit * tiles + t) * TILE, TILE)]
-                pltpu.matmul_push_rhs(ids, staging_register=t % 2, mxu_index=unit, transpose=True)
-            for unit in range(2):
-                block = vbuf[span, pl.ds((unit * tiles + t) * TILE, TILE)]
-                pltpu.matmul_acc_lhs(totals[unit * 2 + i % 2], block, load_staged_rhs=t % 2)
+                block = vbuf[span, pl.ds((2 * t + unit) * TILE, TILE)]
+                pltpu.matmul_acc_lhs(totals[unit * 2 + i % 2], block, load_staged_rhs=n % 2)
 
     def weigh(i):
         netted = pltpu.matmul_pop(totals[i % 2]) + pltpu.matmul_pop(totals[2 + i % 2])
@@ -215,27 +235,53 @@
                 part = term if part is None else part + term
             contrib[path_span, pl.ds(h * LANES, LANES)] = part
 
-    if BARRIER_AFTER < 0:
+    @pl.when(jnp.logical_not(leads))
+    def _():
         meet()
+
+    push(0)
     for i in range(chunks):
-        load(i).wait()
+        load(i, 0).wait()
         if i > 0:
             weigh(i - 1)
-        multiply(i)
+        multiply(i, range(tiles // 2 if i in halved else tiles))
+        if i in halved:
+            load(i, 1).wait()
+            multiply(i, range(tiles // 2, tiles))
         if i == BARRIER_AFTER:
-            meet()
+            @pl.when(leads)
+            def _():
+                meet()
         if i > 0 and i >= BARRIER_AFTER:
-            for j in range(0 if i == BARRIER_AFTER else i - 1, i):
+            for j in range(0 if i == max(BARRIER_AFTER, 1) else i - 1, i):
                 exchange(j)
     weigh(chunks - 1)
     exchange(chunks - 1)
 
-    @pl.when(leads)
-    def _():
-        hazards(1, 0).wait_recv()
-    block = jnp.broadcast_to(jnp.exp(-hbuf[me - core]), (8, paths))
-    pcol[...] = jnp.transpose(block)
-    for q in other_chips:
+    @pl.when(jnp.logical_not(leads))
+    def _():
+        mate_sum[...] = bsum[...]
+    pcol[...] = jnp.transpose(jnp.broadcast_to(jnp.exp(-mate_sum[...]), (8, paths)))
+    @pl.when(leads)
+    def _():
+        pl.semaphore_wait(ready, chips - 1)
+        pl.semaphore_signal(mate, inc=1, device_id=(path_at, partner), device_id_type=MESH)
+        for z in range(n_path - 1):
+            @pl.when(z < path_at)
+            def _():
+                pl.semaphore_signal(above, inc=1, device_id=(z, me), device_id_type=MESH)
+
+    @pl.when(jnp.logical_not(leads))
+    def _():
+        combine(other_chips[0])
+        pl.semaphore_wait(mate, 1)
+        block_copy(other_chips[0], chip).start()
+
+    @pl.when(leads)
+    def _():
+        combine(other_chips[0])
+
+    for q in other_chips[1:]:
         combine(q)
 
         @pl.when(jnp.logical_not(leads))
@@ -259,7 +305,7 @@
         for c in range(1, chips):
             @pl.when(chip == c)
             def _():
-                before_me[...] = sum(hbuf[k] for k in range(2 * c))
+                before_me[...] = sum(hbuf[k] for k in range(c))
         earlier = jnp.broadcast_to(jnp.exp(-before_me[...]), (PACK, paths))
         upper = earlier.astype(bf16).astype(f32)
         at = lax.broadcasted_iota(jnp.int32, (PACK, paths), 0)
@@ -276,7 +322,6 @@
         line = (both[0:1] + both[1:2]) * (1.0 / (paths * n_path))
         for h in range(SETS // LANES):
             row_a[h] = line[:, h * LANES : (h + 1) * LANES]
-        pl.semaphore_wait(ready, n_tm - 1)
         for z in range(n_path - 1):
             @pl.when(z < path_at)
             def _():
@@ -285,6 +330,10 @@
         for other in peers:
             set_row(path_at, other).start()
 
+        for q in other_chips:
+            block_copy(q, chip).start()
+        from_chips(2, chips - 1 - chip)
+        row_copy(hbuf, hbuf, 0, partner).start()
         @pl.when(path_at < n_path - 1)
         def _():
             pl.semaphore_wait(above, n_path - 1 - path_at)
@@ -293,21 +342,15 @@
             def _():
                 for k in range(n_tm):
                     set_row(z, lax.rem(me + 1 + k, n_tm)).start()
-        for q in other_chips:
-            block_copy(q, chip).start()
         rows_a[slot] = row_a[lax.div(flat * share, LANES)]
 
-    from_chips(2, chips - 1 - chip)
-
-    @pl.when(jnp.logical_not(leads))
-    def _():
-        hazards(1, 0).wait_recv()
-        from_chips(1, chip)
+    @pl.when(jnp.logical_not(leads))
+    def _():
+        hazards(chips, 0).wait_recv()
     before = jnp.zeros((1, paths), f32)
     prefix = []
-    for k in range(n_tm):
-        if k % 2 == 0:
-            prefix.append(before)
+    for k in range(chips):
+        prefix.append(before)
         before = before + hbuf[k]
     if chips < 8:
         prefix.append(jnp.zeros((8 - chips, paths), f32))
@@ -335,12 +378,12 @@
     turned = pltpu.roll(sums, lax.rem(LANES - lax.rem(flat * share, LANES), LANES), 1)
     set_out[...] = turned[:1, :share]
 
-    span = hbuf.at[pl.ds(0, n_tm - 1)]
-    remote(span, span, h_send, h_recv.at[0], (path_at, partner)).wait_send()
     blocks.wait_send()
 
     @pl.when(leads)
     def _():
+        hazards(chips, 0).wait_send()
+        hazards(chips - 1, 0).wait_send()
         span = rows_a.at[pl.ds(0, senders - 1)]
         sent = remote(span, span, a_send, a_recv, (path_at, partner))
         sent.wait_send()
@@ -352,6 +395,7 @@
 
     @pl.when(jnp.logical_not(leads))
     def _():
+        row_copy(bsum, mate_sum, 0, partner).wait_send()
         remote(theirs, theirs, p_send, p_recv.at[0], (path_at, partner)).wait_send()
 
 
@@ -397,13 +441,14 @@
                 pltpu.VMEM((n_tm // 2, own, SETS), f32),
                 pltpu.VMEM((1, paths), f32),
                 pltpu.VMEM((1, paths), f32),
-                pltpu.VMEM((n_tm, 1, paths), f32),
+                pltpu.VMEM((1, paths), f32),
+                pltpu.VMEM((n_tm // 2, 1, paths), f32),
                 pltpu.VMEM((paths, 8), f32),
                 pltpu.VMEM((paths, max(8, n_tm // 2)), f32),
                 pltpu.VMEM((2, paths, SETS), jnp.bfloat16),
                 pltpu.VMEM((SETS // LANES, 1, LANES), f32),
                 pltpu.VMEM((n_all // 2, 1, LANES), f32),
-                dma((chunks,)),
+                dma((2 * chunks,)),
                 dma((3,)),
                 dma,
                 dma((3,)),
@@ -413,6 +458,7 @@
                 dma,
                 dma,
                 dma,
+                pltpu.SemaphoreType.REGULAR,
                 pltpu.SemaphoreType.REGULAR,
                 pltpu.SemaphoreType.REGULAR,
             ],

time: 14.1 us -> 14 us (level)
  Pallas kernels: 13.3 us -> 13.1 us
where the time goes in v3:
time: 14 us; the launch traced here: 13.8 us
  Pallas kernels  13.1 us (94%)
  between operations  0.64 us (5%)
    pallas_call x1, Pallas kernels, on_device(): pl.pallas_call(functools.partial(kernel, n_path, n_tm), out_shape=(pltpu....  12.5 us
    pallas_call x1, Pallas kernels, on_device(): pl.pallas_call(finish, out_shape=(jax.ShapeDtypeStruct(pathwise.shape, f3...  0.65 us

profile of v3, /device:TPU:0, one launch (start us, length us, event | category | flops | bytes accessed | tf_op | source)
XLA Modules:
  0.0 13.8 jit_solution(2860452583306574660)
XLA Ops:
  0.6 12.5 %shard_map.59 = (f32[64,256]{1,0:T(8,128)S(1)}, f32[1,8]{1,0:T(1,128)S(1)}) custom-call(bf16[512,2,2048]{2,1,0:T(2,128)(2,1)} %refs_0_.1, f32[2,512]{1,0:T(2,128)} %refs_1_.1, f32[2]{0:T(128)} %refs_2_.1, s32[16,128]{1,0:T(8,128)} %bitcast.2), custom_call_target="tpu_custom_call" | custom-call | tf_op jit(solution)/shard_map/pallas_call | solution.py:425
  13.1 0.7 %shard_map.60 = (f32[64,256]{1,0:T(8,128)}, f32[1,8]{1,0:T(1,128)}) custom-call(f32[64,256]{1,0:T(8,128)S(1)} %get-tuple-element.6.pathwise, f32[1,8]{1,0:T(1,128)S(1)} %get-tuple-element.7.sets), custom_call_target="tpu_custom_call" | custom-call | tf_op jit(solution)/shard_map/pallas_call | solution.py:471

commit v4 on v3

--- a/solution.py
+++ b/solution.py
@@ -20,13 +20,14 @@
     rows = CHUNK_PATHS * refs[0].shape[1]
     sums = [pltpu.ACC(unit)((rows, SETS), jnp.float32) for unit in (0, 0, 1, 1)]
     sums += [pltpu.ACC(unit)((PACK, SETS), jnp.float32) for unit in (0, 1)]
+    sums += [pltpu.ACC(unit)((rows // 2, SETS), jnp.float32) for unit in (0, 0, 1, 1)]
     pl.run_scoped(lambda *totals: body(n_path, n_tm, totals, *refs), *sums)
 
 
 def body(
     n_path, n_tm, totals, values, hazard_in, spread_in, trade_in, out, set_out,
-    vbuf, ts, oh, hz, spread, nbuf, wt, contrib, theirs, comb, recv, bsum, mate_sum, before_me, hbuf, pcol, ecol, limbs, row_a, rows_a,
-    load_sem, small_sem, h_send, h_recv, p_send, p_recv, b_send, b_recv, a_send, a_recv, mate, ready, above,
+    vbuf, ts, oh, hz, spread, nbuf, wt, contrib, theirs, comb, recv, bsum, mate_sum, before_me, erow, hbuf, pcol, ecol, limbs, row_a, rows_a,
+    load_sem, small_sem, h_recv, p_recv, b_recv, a_recv, mate, ready, above,
 ):
     paths, dates, trades = values.shape
     f32, bf16 = jnp.float32, jnp.bfloat16
@@ -54,16 +55,16 @@
         first = [lax.rem(my_chunk + 1 + i, chunks) for i in range(chunks)]
     flat_values = values.reshape(paths * dates, trades)
 
-    half = trades // 2
-    halved = tuple(range(chunks))
+    last = chunks - 1
+    h_send, p_send, b_send, a_send = small_sem.at[0], load_sem.at[0], load_sem.at[1], load_sem.at[2]
 
     def load(i, part):
-        span = pl.ds(pl.multiple_of(first[i] * rows, rows), rows)
-        at = i + sum(j < i for j in halved) + part
-        if i in halved:
-            area = (span, pl.ds(part * half, half))
-            return pltpu.make_async_copy(flat_values.at[area], vbuf.at[area], load_sem.at[at])
-        return pltpu.make_async_copy(flat_values.at[span], vbuf.at[span], load_sem.at[at])
+        begin = pl.multiple_of(first[i] * rows, rows)
+        if i == last:
+            area = (pl.ds(pl.multiple_of(begin + part * rows // 2, rows // 2), rows // 2), slice(None))
+        else:
+            area = (pl.ds(begin, rows), pl.ds(part * trades // 2, trades // 2))
+        return pltpu.make_async_copy(flat_values.at[area], vbuf.at[area], load_sem.at[2 * i + part])
 
     barrier = pltpu.get_barrier_semaphore()
     pl.semaphore_signal(barrier, inc=1, device_id=(path_at, partner), device_id_type=MESH)
@@ -73,16 +74,15 @@
         for other in lead_peers:
             pl.semaphore_signal(barrier, inc=1, device_id=(path_at, other), device_id_type=MESH)
 
-    copy_trades = pltpu.make_async_copy(trade_in, ts, small_sem.at[0])
-    copy_hazard = pltpu.make_async_copy(hazard_in, hz, small_sem.at[1])
+    copy_hazard = pltpu.make_async_copy(hazard_in, hz, small_sem.at[0])
+    copy_trades = pltpu.make_async_copy(trade_in, ts, small_sem.at[1])
     copy_spread = pltpu.make_async_copy(spread_in, spread, small_sem.at[2])
+    copy_hazard.start()
     copy_trades.start()
-    copy_hazard.start()
     copy_spread.start()
     for i in range(chunks):
-        load(i, 0).start()
-        if i in halved:
-            load(i, 1).start()
+        for part in range(2):
+            load(i, part).start()
     for z in range(1, n_path):
         @pl.when(z > path_at)
         def _():
@@ -138,6 +138,31 @@
         span = rows_a.at[pl.ds(0, count)]
         return remote(span, span, a_send, a_recv, (path_at, partner))
 
+    copy_hazard.wait()
+    bsum[...] = sum(hz[pl.ds(d, 1), :] for d in range(dates))
+
+    def meet():
+        pl.semaphore_wait(barrier, 1 + path_at + core * (chips - 1))
+
+        @pl.when(jnp.logical_not(leads))
+        def _():
+            row_copy(bsum, mate_sum, 0, partner).start()
+            pl.semaphore_signal(mate, inc=1, device_id=(path_at, partner), device_id_type=MESH)
+
+        @pl.when(leads)
+        def _():
+            pl.semaphore_wait(mate, 1)
+            for other in lead_peers:
+                pl.semaphore_signal(ready, inc=1, device_id=(path_at, other), device_id_type=MESH)
+            row_copy(bsum, mate_sum, 0, partner).wait_recv()
+            hbuf[chip] = bsum[...] + mate_sum[...]
+            for k in range(1, chips):
+                there = lax.rem(chip + k, chips)
+                row_copy(hbuf.at[chip], hbuf.at[chip], jnp.where(there > chip, 1, 2), there * 2 + 1).start()
+
+    @pl.when(jnp.logical_not(leads))
+    def _():
+        meet()
     copy_trades.wait()
     base = lax.broadcasted_iota(jnp.int32, (PACK, LANES), 0)
     set_at = [(base + PACK * r).astype(f32).astype(bf16) for r in range(SETS // PACK)]
@@ -148,7 +173,6 @@
             picked = jnp.where(ids == set_at[r], one, zero)
             oh[pl.ds(r * PACK, PACK), pl.ds(block * LANES, LANES)] = picked.astype(oh.dtype)
 
-    copy_hazard.wait()
     copy_spread.wait()
     total = jnp.zeros((1, paths), f32)
     weight_rows = []
@@ -158,30 +182,26 @@
         weight_rows.append((spread[d] * scale) * jnp.exp(-total))
     weight_rows.append(jnp.zeros((8 - dates, paths), f32))
     wt[...] = jnp.transpose(jnp.concatenate(weight_rows, axis=0))
-    bsum[...] = total
-
-    def meet():
-        pl.semaphore_wait(barrier, 1 + path_at + core * (chips - 1))
-
-        @pl.when(jnp.logical_not(leads))
-        def _():
-            row_copy(bsum, mate_sum, 0, partner).start()
-            pl.semaphore_signal(mate, inc=1, device_id=(path_at, partner), device_id_type=MESH)
-
-        @pl.when(leads)
-        def _():
-            pl.semaphore_wait(mate, 1)
-            for other in lead_peers:
-                pl.semaphore_signal(ready, inc=1, device_id=(path_at, other), device_id_type=MESH)
-            row_copy(bsum, mate_sum, 0, partner).wait_recv()
-            hbuf[chip] = bsum[...] + mate_sum[...]
-            for k in range(1, chips):
-                there = lax.rem(chip + k, chips)
-                row_copy(hbuf.at[chip], hbuf.at[chip], jnp.where(there > chip, 1, 2), there * 2 + 1).start()
 
     def exchange(i):
         for k in range(per // 2):
             per_core(first[i] * (per // 2) + k, lambda q, send, take: pair_copy(q, send).start())
+
+    def exchange_half(part):
+        chips_here = per // 2
+        if chips_here > 1:
+            for k in range(part * chips_here // 2, (part + 1) * chips_here // 2):
+                per_core(first[last] * chips_here + k, lambda q, send, take: pair_copy(q, send).start())
+            return
+
+        @pl.when(jnp.logical_not(leads))
+        def _():
+            pair_copy(my_chunk, own_rows(my_chunk * 2 + part)).start()
+
+        if part == 0:
+            @pl.when(leads)
+            def _():
+                pair_copy(my_chunk, own_rows(my_chunk * 2)).start()
 
     def combine(q):
         per_core(q, lambda q, send, take: pair_copy(q, take).wait_recv())
@@ -211,52 +231,64 @@
             ids = oh[:, pl.ds((2 * (n % tiles) + unit) * TILE, TILE)]
             pltpu.matmul_push_rhs(ids, staging_register=n % 2, mxu_index=unit, transpose=True)
 
-    def multiply(i, steps):
-        span = pl.ds(pl.multiple_of(first[i] * rows, rows), rows)
+    def multiply(n, span, into, steps):
         for t in steps:
-            n = i * tiles + t
-            if n + 1 < chunks * tiles:
-                push(n + 1)
+            if n + t + 1 < (chunks + 1) * tiles:
+                push(n + t + 1)
             for unit in range(2):
                 block = vbuf[span, pl.ds((2 * t + unit) * TILE, TILE)]
-                pltpu.matmul_acc_lhs(totals[unit * 2 + i % 2], block, load_staged_rhs=n % 2)
-
-    def weigh(i):
-        netted = pltpu.matmul_pop(totals[i % 2]) + pltpu.matmul_pop(totals[2 + i % 2])
+                pltpu.matmul_acc_lhs(into[unit], block, load_staged_rhs=(n + t) % 2)
+
+    def weigh(i, begin, paths_here, done):
+        netted = pltpu.matmul_pop(done[0]) + pltpu.matmul_pop(done[1])
         for h in range(SETS // LANES):
-            nbuf[i, h] = netted[:, h * LANES : (h + 1) * LANES]
-        path_span = chunk_span(i)
+            nbuf[i, h, pl.ds(begin * dates, paths_here * dates)] = netted[:, h * LANES : (h + 1) * LANES]
+        path_span = pl.ds(pl.multiple_of(first[i] * CHUNK_PATHS + begin, paths_here), paths_here)
         weight = wt[path_span, :]
         for h in range(SETS // LANES):
             part = None
             for d in range(dates):
-                picked = nbuf[i, h, pl.ds(d, CHUNK_PATHS, stride=dates), :]
+                picked = nbuf[i, h, pl.ds(begin * dates + d, paths_here, stride=dates), :]
                 term = weight[:, d : d + 1] * jnp.maximum(picked, 0.0)
                 part = term if part is None else part + term
             contrib[path_span, pl.ds(h * LANES, LANES)] = part
 
-    @pl.when(jnp.logical_not(leads))
-    def _():
-        meet()
-
+    def whole(i):
+        return totals[i % 2], totals[2 + i % 2]
+
+    def in_half(part):
+        return totals[6 + part], totals[8 + part]
+
+    some = CHUNK_PATHS // 2
     push(0)
     for i in range(chunks):
-        load(i, 0).wait()
-        if i > 0:
-            weigh(i - 1)
-        multiply(i, range(tiles // 2 if i in halved else tiles))
-        if i in halved:
-            load(i, 1).wait()
-            multiply(i, range(tiles // 2, tiles))
-        if i == BARRIER_AFTER:
-            @pl.when(leads)
-            def _():
-                meet()
-        if i > 0 and i >= BARRIER_AFTER:
-            for j in range(0 if i == max(BARRIER_AFTER, 1) else i - 1, i):
-                exchange(j)
-    weigh(chunks - 1)
-    exchange(chunks - 1)
+        for part in range(2):
+            load(i, part).wait()
+            if part == 0 and i > 0:
+                weigh(i - 1, 0, CHUNK_PATHS, whole(i - 1))
+            if i < last:
+                span = pl.ds(pl.multiple_of(first[i] * rows, rows), rows)
+                steps = range(part * tiles // 2, (part + 1) * tiles // 2)
+                multiply(i * tiles, span, whole(i), steps)
+            else:
+                if part == 1:
+                    weigh(i, 0, some, in_half(0))
+                begin = pl.multiple_of(first[i] * rows + part * rows // 2, rows // 2)
+                multiply((i + part) * tiles, pl.ds(begin, rows // 2), in_half(part), range(tiles))
+            if i == BARRIER_AFTER and part == 1:
+                @pl.when(leads)
+                def _():
+                    meet()
+            if i == last:
+                if part == 0:
+                    exchange(last - 1)
+                else:
+                    exchange_half(0)
+            elif part == 1 and i > 0 and i >= BARRIER_AFTER:
+                for j in range(0 if i == max(BARRIER_AFTER, 1) else i - 1, i):
+                    exchange(j)
+    weigh(last, some, some, in_half(1))
+    exchange_half(1)
 
     @pl.when(jnp.logical_not(leads))
     def _():
@@ -288,18 +320,8 @@
         def _():
             block_copy(q, chip).start()
 
-    combine(own_chips[0])
-
-    def limb(unit, t, part):
-        block = limbs[part, pl.ds((unit * row_tiles + t) * TILE, TILE), :]
-        pltpu.matmul_push_rhs(block, staging_register=part, mxu_index=unit)
-
-    row_tiles = paths // TILE // 2
-    @pl.when(leads)
-    def _():
-        for unit in range(2):
-            for part in range(2):
-                limb(unit, 0, part)
+    @pl.when(leads)
+    def _():
         from_chips(1, chip)
         before_me[...] = jnp.zeros((1, paths), f32)
         for c in range(1, chips):
@@ -309,7 +331,20 @@
         earlier = jnp.broadcast_to(jnp.exp(-before_me[...]), (PACK, paths))
         upper = earlier.astype(bf16).astype(f32)
         at = lax.broadcasted_iota(jnp.int32, (PACK, paths), 0)
-        weights = jnp.where(at == 0, upper, jnp.where(at == 1, earlier - upper, 0.0)).astype(bf16)
+        erow[...] = jnp.where(at == 0, upper, jnp.where(at == 1, earlier - upper, 0.0)).astype(bf16)
+
+    combine(own_chips[0])
+
+    def limb(unit, t, part):
+        block = limbs[part, pl.ds((unit * row_tiles + t) * TILE, TILE), :]
+        pltpu.matmul_push_rhs(block, staging_register=part, mxu_index=unit)
+
+    row_tiles = paths // TILE // 2
+    @pl.when(leads)
+    def _():
+        for unit in range(2):
+            for part in range(2):
+                limb(unit, 0, part)
         for t in range(row_tiles):
             for unit in range(2):
                 if t > 0:
@@ -317,7 +352,7 @@
                     limb(unit, t, 1)
                 begin = (unit * row_tiles + t) * TILE
                 for part in range(2):
-                    pltpu.matmul_acc_lhs(totals[4 + unit], weights[:, begin : begin + TILE], load_staged_rhs=part)
+                    pltpu.matmul_acc_lhs(totals[4 + unit], erow[:, pl.ds(begin, TILE)], load_staged_rhs=part)
         both = pltpu.matmul_pop(totals[4]) + pltpu.matmul_pop(totals[5])
         line = (both[0:1] + both[1:2]) * (1.0 / (paths * n_path))
         for h in range(SETS // LANES):
@@ -442,6 +477,7 @@
                 pltpu.VMEM((1, paths), f32),
                 pltpu.VMEM((1, paths), f32),
                 pltpu.VMEM((1, paths), f32),
+                pltpu.VMEM((PACK, paths), jnp.bfloat16),
                 pltpu.VMEM((n_tm // 2, 1, paths), f32),
                 pltpu.VMEM((paths, 8), f32),
                 pltpu.VMEM((paths, max(8, n_tm // 2)), f32),
@@ -450,12 +486,8 @@
                 pltpu.VMEM((n_all // 2, 1, LANES), f32),
                 dma((2 * chunks,)),
                 dma((3,)),
-                dma,
                 dma((3,)),
-                dma,
                 dma((n_tm // 2,)),
-                dma,
-                dma,
                 dma,
                 dma,
                 pltpu.SemaphoreType.REGULAR,

time: 14 us -> 13.7 us (0.979)
  Pallas kernels: 13.1 us -> 12.9 us
    pallas_call x1, Pallas kernels: 12.5 us -> 12.3 us  [on_device(): pl.pallas_call(functools.partial(kernel, n_path, n_tm), out_shape=(pltpu....]
where the time goes in v4:
time: 13.7 us; the launch traced here: 13.6 us
  Pallas kernels  12.9 us (94%)
  between operations  0.64 us (5%)
    pallas_call x1, Pallas kernels, on_device(): pl.pallas_call(functools.partial(kernel, n_path, n_tm), out_shape=(pltpu....  12.3 us
    pallas_call x1, Pallas kernels, on_device(): pl.pallas_call(finish, out_shape=(jax.ShapeDtypeStruct(pathwise.shape, f3...  0.65 us

profile of v4, /device:TPU:0, one launch (start us, length us, event | category | flops | bytes accessed | tf_op | source)
XLA Modules:
  0.0 13.6 jit_solution(11245115440066704690)
XLA Ops:
  0.6 12.3 %shard_map.59 = (f32[64,256]{1,0:T(8,128)S(1)}, f32[1,8]{1,0:T(1,128)S(1)}) custom-call(bf16[512,2,2048]{2,1,0:T(2,128)(2,1)} %refs_0_.1, f32[2,512]{1,0:T(2,128)} %refs_1_.1, f32[2]{0:T(128)} %refs_2_.1, s32[16,128]{1,0:T(8,128)} %bitcast.2), custom_call_target="tpu_custom_call" | custom-call | tf_op jit(solution)/shard_map/pallas_call | solution.py:460
  12.9 0.7 %shard_map.60 = (f32[64,256]{1,0:T(8,128)}, f32[1,8]{1,0:T(1,128)}) custom-call(f32[64,256]{1,0:T(8,128)S(1)} %get-tuple-element.6.pathwise, f32[1,8]{1,0:T(1,128)S(1)} %get-tuple-element.7.sets), custom_call_target="tpu_custom_call" | custom-call | tf_op jit(solution)/shard_map/pallas_call | solution.py:503

commit v5 on v4

--- a/solution.py
+++ b/solution.py
@@ -361,7 +361,7 @@
             @pl.when(z < path_at)
             def _():
                 for k in range(n_tm):
-                    set_row(z, lax.rem(me + 1 + k, n_tm)).start()
+                    set_row(z, k).start()
         for other in peers:
             set_row(path_at, other).start()
 
@@ -376,7 +376,7 @@
             @pl.when(z > path_at)
             def _():
                 for k in range(n_tm):
-                    set_row(z, lax.rem(me + 1 + k, n_tm)).start()
+                    set_row(z, k).start()
         rows_a[slot] = row_a[lax.div(flat * share, LANES)]
 
     @pl.when(jnp.logical_not(leads))
@@ -409,9 +409,17 @@
     @pl.when(jnp.logical_not(leads))
     def _():
         set_rows(senders).wait_recv()
-    sums = jnp.broadcast_to(jnp.sum(rows_a[...], axis=0), (8, LANES))
-    turned = pltpu.roll(sums, lax.rem(LANES - lax.rem(flat * share, LANES), LANES), 1)
-    set_out[...] = turned[:1, :share]
+    sums = jnp.sum(rows_a[...], axis=0)
+    shift = lax.rem(flat * share, LANES)
+
+    @pl.when(shift == 0)
+    def _():
+        set_out[...] = sums[:, :share]
+
+    @pl.when(shift != 0)
+    def _():
+        turned = pltpu.roll(jnp.broadcast_to(sums, (8, LANES)), lax.rem(LANES - shift, LANES), 1)
+        set_out[...] = turned[:1, :share]
 
     blocks.wait_send()
 

time: 13.7 us -> 13.7 us (level)
  no operation moved by 1% of the time
where the time goes in v5:
time: 13.7 us; the launch traced here: 13.5 us
  Pallas kernels  12.8 us (93%)
  between operations  0.64 us (5%)
    pallas_call x1, Pallas kernels, on_device(): pl.pallas_call(functools.partial(kernel, n_path, n_tm), out_shape=(pltpu....  12.2 us
    pallas_call x1, Pallas kernels, on_device(): pl.pallas_call(finish, out_shape=(jax.ShapeDtypeStruct(pathwise.shape, f3...  0.65 us

profile of v5, /device:TPU:0, one launch (start us, length us, event | category | flops | bytes accessed | tf_op | source)
XLA Modules:
  0.0 13.5 jit_solution(12892050069455273236)
XLA Ops:
  0.6 12.2 %shard_map.59 = (f32[64,256]{1,0:T(8,128)S(1)}, f32[1,8]{1,0:T(1,128)S(1)}) custom-call(bf16[512,2,2048]{2,1,0:T(2,128)(2,1)} %refs_0_.1, f32[2,512]{1,0:T(2,128)} %refs_1_.1, f32[2]{0:T(128)} %refs_2_.1, s32[16,128]{1,0:T(8,128)} %bitcast.2), custom_call_target="tpu_custom_call" | custom-call | tf_op jit(solution)/shard_map/pallas_call | solution.py:468
  12.8 0.7 %shard_map.60 = (f32[64,256]{1,0:T(8,128)}, f32[1,8]{1,0:T(1,128)}) custom-call(f32[64,256]{1,0:T(8,128)S(1)} %get-tuple-element.6.pathwise, f32[1,8]{1,0:T(1,128)S(1)} %get-tuple-element.7.sets), custom_call_target="tpu_custom_call" | custom-call | tf_op jit(solution)/shard_map/pallas_call | solution.py:511

commit v6 on v5

--- a/solution.py
+++ b/solution.py
@@ -204,12 +204,17 @@
                 pair_copy(my_chunk, own_rows(my_chunk * 2)).start()
 
     def combine(q):
+        @pl.when(leads)
+        def _():
+            span = both_rows(q)
+            comb[span, :] = pcol[span, 0:1] * contrib[span, :]
+
         per_core(q, lambda q, send, take: pair_copy(q, take).wait_recv())
 
         @pl.when(leads)
         def _():
             span = both_rows(q)
-            both = theirs[span, :] + pcol[span, 0:1] * contrib[span, :]
+            both = theirs[span, :] + comb[span, :]
             comb[span, :] = both
             upper = both.astype(bf16)
             limbs[0, span, :] = upper

time: 13.7 us -> 13.6 us (level)
  no operation moved by 1% of the time
where the time goes in v6:
time: 13.6 us; the launch traced here: 13.4 us
  Pallas kernels  12.8 us (94%)
  between operations  0.64 us (5%)
    pallas_call x1, Pallas kernels, on_device(): pl.pallas_call(functools.partial(kernel, n_path, n_tm), out_shape=(pltpu....  12.1 us
    pallas_call x1, Pallas kernels, on_device(): pl.pallas_call(finish, out_shape=(jax.ShapeDtypeStruct(pathwise.shape, f3...  0.65 us

profile of v6, /device:TPU:0, one launch (start us, length us, event | category | flops | bytes accessed | tf_op | source)
XLA Modules:
  0.0 13.4 jit_solution(10037065180957754482)
XLA Ops:
  0.6 12.1 %shard_map.59 = (f32[64,256]{1,0:T(8,128)S(1)}, f32[1,8]{1,0:T(1,128)S(1)}) custom-call(bf16[512,2,2048]{2,1,0:T(2,128)(2,1)} %refs_0_.1, f32[2,512]{1,0:T(2,128)} %refs_1_.1, f32[2]{0:T(128)} %refs_2_.1, s32[16,128]{1,0:T(8,128)} %bitcast.2), custom_call_target="tpu_custom_call" | custom-call | tf_op jit(solution)/shard_map/pallas_call | solution.py:473
  12.8 0.7 %shard_map.60 = (f32[64,256]{1,0:T(8,128)}, f32[1,8]{1,0:T(1,128)}) custom-call(f32[64,256]{1,0:T(8,128)S(1)} %get-tuple-element.6.pathwise, f32[1,8]{1,0:T(1,128)S(1)} %get-tuple-element.7.sets), custom_call_target="tpu_custom_call" | custom-call | tf_op jit(solution)/shard_map/pallas_call | solution.py:516
